TPU v7x, 32 devices: a whole 2x2x4 slice. The times are simulated.
32 devices in a mesh: rep: 4 (over z), seq: 8 (over y, x, core).
Axes of the slice: x: 2, y: 2, z: 4, core: 2. Of those that a mesh axis runs over, the one named last changes fastest.
Arguments:
- frames_in: bfloat16 [4, 8, 4, 128, 1152], P('rep', 'seq'), may hold values from -6 to 6
- conditioning: float32 [4, 1152], P('rep'), may hold values from -6 to 6
- mod_first: bfloat16 [1152, 6912], P('seq'), may hold values from -0.1875 to 0.1875
- qkv_first: bfloat16 [1152, 3456], P('seq'), may hold values from -0.1875 to 0.1875
- out_first: bfloat16 [1152, 1152], P('seq'), may hold values from -0.75 to 0.75
- up_first: bfloat16 [1152, 4608], P('seq'), may hold values from -0.1875 to 0.1875
- down_first: bfloat16 [4608, 1152], P('seq'), may hold values from -0.09375 to 0.09375
- mod_second: bfloat16 [1152, 6912], P('seq'), may hold values from -0.1875 to 0.1875
- qkv_second: bfloat16 [1152, 3456], P('seq'), may hold values from -0.1875 to 0.1875
- out_second: bfloat16 [1152, 1152], P('seq'), may hold values from -0.375 to 0.375
- up_second: bfloat16 [1152, 4608], P('seq'), may hold values from -0.1875 to 0.1875
- down_second: bfloat16 [4608, 1152], P('seq'), may hold values from -0.09375 to 0.09375
- cotangent: float32 [4, 8, 4, 128, 1152], P('rep', 'seq'), may hold values from -6 to 6
Outputs:
- block_out: float32 [4, 8, 4, 128, 1152], P('rep', 'seq')
- input_grad: float32 [4, 8, 4, 128, 1152], P('rep', 'seq')
- conditioning_grad: float32 [4, 1152], P('rep', 'seq')
- mod_first_grad: float32 [1152, 6912], P('seq')
- qkv_first_grad: float32 [1152, 3456], P('seq')
- out_first_grad: float32 [1152, 1152], P('seq')
- up_first_grad: float32 [1152, 4608], P('seq')
- first_down_gradient: float32 [4608, 1152], P('seq')
- mod_second_grad: float32 [1152, 6912], P('seq')
- qkv_second_grad: float32 [1152, 3456], P('seq')
- out_second_grad: float32 [1152, 1152], P('seq')
- up_second_grad: float32 [1152, 4608], P('seq')
- down_second_grad: float32 [4608, 1152], P('seq')
All inputs are finite; a program needn't handle non-finite values.
Results may differ from a plain program's by a relative error of at most 0.02175.
Values may be sent and summed in bfloat16 or wider, within the bound.
A program may use at most 384 MiB of HBM per device.

v0:
```python
import jax
import jax.numpy as jnp
from jax import lax
from jax.sharding import PartitionSpec as P

HEADS = 16
HEAD_WIDTH = 72
norm_epsilon = 1e-06


def from_partner(block, axis, apart):
    count = lax.axis_size(axis)
    route = []
    for low in range(count):
        high = low | 1 << apart
        if high != low and high < count:
            route += [(low, high), (high, low)]
    return lax.ppermute(block, axis, route)


def shortened(x):
    return jax.tree.map(lambda a: a.astype(jnp.bfloat16) if a.dtype == jnp.float32 else a, x)


def layer_mod(stream, shift_part, scale_part):
    row_mean = jnp.mean(stream, axis=-1, keepdims=True)
    centred = stream - row_mean
    row_var = jnp.mean(centred * centred, axis=-1, keepdims=True)
    return centred * lax.rsqrt(row_var + norm_epsilon) * (1.0 + scale_part) + shift_part


def gelu_tanh(pre_value):
    return jax.nn.gelu(pre_value, approximate=True)


def project(left_operand, right_operand):
    return jnp.einsum(
        "csld,de->csle", left_operand, right_operand, preferred_element_type=jnp.float32
    )


def project_back(incoming, right_operand):
    return jnp.einsum("csle,de->csld", incoming, right_operand, preferred_element_type=jnp.float32)


def mod_parts(modulation):
    return [segment[:, None, None, :] for segment in jnp.split(modulation, 6, axis=-1)]


def modulations(conditioning, mod_one, mod_two):
    row_count = mod_one.shape[0]
    row_start = lax.axis_index("seq") * row_count
    silu_local = lax.dynamic_slice_in_dim(
        jax.nn.silu(conditioning), row_start, row_count, 1
    ).astype(jnp.bfloat16)
    part_one = jnp.dot(silu_local, mod_one, preferred_element_type=jnp.float32)
    part_two = jnp.dot(silu_local, mod_two, preferred_element_type=jnp.float32)
    summed = lax.psum((part_one, part_two), "seq")
    return (summed[0], summed[1], silu_local, row_start)


def gather_layer(qkv_w, out_w, up_w, down_w):
    return (
        lax.all_gather(qkv_w, "seq", axis=0, tiled=True),
        lax.all_gather(out_w, "seq", axis=0, tiled=True),
        lax.all_gather(up_w, "seq", axis=0, tiled=True),
        lax.all_gather(down_w, "seq", axis=0, tiled=True),
    )


def gather_layer_again(qkv_w, out_w, up_w, down_w):
    return (
        lax.all_gather(qkv_w, "seq", axis=0, tiled=True),
        lax.all_gather(out_w, "seq", axis=0, tiled=True),
        lax.all_gather(up_w, "seq", axis=0, tiled=True),
        lax.all_gather(down_w, "seq", axis=0, tiled=True),
    )


def partner_values(stacked):
    return from_partner(stacked, "seq", 0)


def partner_grads(stacked):
    return from_partner(stacked.astype(jnp.bfloat16), "seq", 0).astype(stacked.dtype)


def to_places(stream):
    clip_count, frame_dev, half_places, features = stream.shape
    devices = lax.axis_size("seq")
    place_part = half_places // devices
    exchanged = lax.all_to_all(
        stream.reshape(1, clip_count, frame_dev, devices, place_part, features).astype(
            jnp.bfloat16
        ),
        "seq",
        split_axis=3,
        concat_axis=0,
        tiled=True,
    ).astype(jnp.float32)
    exchanged = exchanged.reshape(devices // 2, 2, clip_count, frame_dev, place_part, features)
    exchanged = jnp.transpose(exchanged, (2, 1, 4, 0, 3, 5))
    return exchanged.reshape(clip_count, 2 * place_part, devices // 2 * frame_dev, features)


def to_frames(stream, frame_dev):
    clip_count, place_count, frame_total, features = stream.shape
    devices = lax.axis_size("seq")
    place_part = place_count // 2
    arranged = stream.reshape(clip_count, 2, place_part, devices // 2, frame_dev, features)
    arranged = jnp.transpose(arranged, (3, 1, 0, 4, 2, 5)).reshape(
        devices, clip_count, frame_dev, 1, place_part, features
    )
    exchanged = lax.all_to_all(
        shortened(arranged), "seq", split_axis=0, concat_axis=3, tiled=True
    ).astype(arranged.dtype)
    return exchanged.reshape(clip_count, frame_dev, devices * place_part, features)


def forward_layer(stream, modulation, weights, spatial):
    qkv_w, out_w, up_w, down_w = weights
    shift_attn, scale_attn, gate_attn, shift_mlp, scale_mlp, gate_mlp = mod_parts(modulation)
    clip_count, seq_count, seq_len, features = stream.shape
    normed = layer_mod(stream, shift_attn, scale_attn).astype(jnp.bfloat16)
    projected = project(normed, qkv_w).astype(jnp.bfloat16)
    queries, keys_all, values_all = jnp.split(projected, 3, axis=-1)
    if spatial:
        remote = partner_values(jnp.stack([keys_all, values_all]))
        keys_all = jnp.concatenate([keys_all, remote[0]], axis=2)
        values_all = jnp.concatenate([values_all, remote[1]], axis=2)
    key_len = keys_all.shape[2]
    queries = queries.reshape(clip_count, seq_count, seq_len, HEADS, HEAD_WIDTH)
    keys_all = keys_all.reshape(clip_count, seq_count, key_len, HEADS, HEAD_WIDTH)
    values_all = values_all.reshape(clip_count, seq_count, key_len, HEADS, HEAD_WIDTH)
    scores = jnp.einsum(
        "cslhe,csmhe->cshlm", queries, keys_all, preferred_element_type=jnp.float32
    ) * HEAD_WIDTH ** (-0.5)
    peak_score = jnp.max(scores, axis=-1, keepdims=True)
    scaled_exp = jnp.exp(scores - peak_score)
    attention = scaled_exp / jnp.sum(scaled_exp, axis=-1, keepdims=True)
    attention_low = attention.astype(jnp.bfloat16)
    attended = jnp.einsum(
        "cshlm,csmhe->cslhe", attention_low, values_all, preferred_element_type=jnp.float32
    )
    attended = attended.astype(jnp.bfloat16).reshape(clip_count, seq_count, seq_len, features)
    branch = project(attended, out_w)
    middle = stream + gate_attn * branch
    normed_mid = layer_mod(middle, shift_mlp, scale_mlp).astype(jnp.bfloat16)
    hidden_pre = project(normed_mid, up_w)
    hidden = gelu_tanh(hidden_pre).astype(jnp.bfloat16)
    mlp_out = project(hidden, down_w)
    result = middle + gate_mlp * mlp_out
    kept_state = (
        normed,
        queries,
        keys_all,
        values_all,
        attention,
        attention_low,
        attended,
        branch,
        middle,
        normed_mid,
        hidden_pre,
        hidden,
        mlp_out,
    )
    return (result, kept_state)


def backward_layer(result_grad, stream, modulation, weights, kept_state, spatial):
    qkv_w, out_w, up_w, down_w = weights
    (
        normed,
        queries,
        keys_all,
        values_all,
        attention,
        attention_low,
        attended,
        branch,
        middle,
        normed_mid,
        hidden_pre,
        hidden,
        mlp_out,
    ) = kept_state
    shift_attn, scale_attn, gate_attn, shift_mlp, scale_mlp, gate_mlp = mod_parts(modulation)
    clip_count, seq_count, seq_len, features = stream.shape
    gate_mlp_grad = jnp.sum(result_grad * mlp_out, axis=(1, 2))
    mlp_grad = (gate_mlp * result_grad).astype(jnp.bfloat16)
    hidden_grad = project_back(mlp_grad, down_w)
    pre_grad = jax.vjp(gelu_tanh, hidden_pre)[1](hidden_grad)[0].astype(jnp.bfloat16)
    normed_mid_grad = project_back(pre_grad, up_w)
    middle_ln_grad, shift_mlp_grad, scale_mlp_grad = jax.vjp(
        layer_mod, middle, shift_mlp, scale_mlp
    )[1](normed_mid_grad)
    middle_grad = result_grad + middle_ln_grad
    gate_attn_grad = jnp.sum(middle_grad * branch, axis=(1, 2))
    branch_grad = (gate_attn * middle_grad).astype(jnp.bfloat16)
    attended_grad = project_back(branch_grad, out_w).astype(jnp.bfloat16)
    attended_grad = attended_grad.reshape(clip_count, seq_count, seq_len, HEADS, HEAD_WIDTH)
    attention_grad = jnp.einsum(
        "cslhe,csmhe->cshlm", attended_grad, values_all, preferred_element_type=jnp.float32
    )
    scores_grad = attention * (
        attention_grad - jnp.sum(attention_grad * attention, axis=-1, keepdims=True)
    )
    scores_grad = scores_grad.astype(jnp.bfloat16)
    inv_root = HEAD_WIDTH ** (-0.5)
    queries_grad = (
        jnp.einsum("cshlm,csmhe->cslhe", scores_grad, keys_all, preferred_element_type=jnp.float32)
        * inv_root
    )
    keys_grad = (
        jnp.einsum("cshlm,cslhe->csmhe", scores_grad, queries, preferred_element_type=jnp.float32)
        * inv_root
    )
    values_grad = jnp.einsum(
        "cshlm,cslhe->csmhe", attention_low, attended_grad, preferred_element_type=jnp.float32
    )
    if spatial:
        returned = partner_grads(
            jnp.stack([keys_grad[:, :, seq_len:], values_grad[:, :, seq_len:]])
        )
        keys_grad = keys_grad[:, :, :seq_len] + returned[0]
        values_grad = values_grad[:, :, :seq_len] + returned[1]
    qkv_grad = jnp.concatenate(
        [
            component.reshape(clip_count, seq_count, seq_len, features)
            for component in (queries_grad, keys_grad, values_grad)
        ],
        axis=-1,
    )
    qkv_grad = qkv_grad.astype(jnp.bfloat16)
    normed_grad = project_back(qkv_grad, qkv_w)
    stream_ln_grad, attention_shift_gradient, scale_attn_grad = jax.vjp(
        layer_mod, stream, shift_attn, scale_attn
    )[1](normed_grad)
    stream_grad = middle_grad + stream_ln_grad
    mod_grad = jnp.concatenate(
        [
            attention_shift_gradient.reshape(clip_count, features),
            scale_attn_grad.reshape(clip_count, features),
            gate_attn_grad,
            shift_mlp_grad.reshape(clip_count, features),
            scale_mlp_grad.reshape(clip_count, features),
            gate_mlp_grad,
        ],
        axis=-1,
    )
    grad_pairs = (
        (normed, qkv_grad),
        (attended, branch_grad),
        (normed_mid, pre_grad),
        (hidden, mlp_grad),
    )
    return (stream_grad, mod_grad, grad_pairs)


def spread_rows_out(left_operand, right_operand):
    left_flat = left_operand.reshape(-1, left_operand.shape[-1])
    right_flat = right_operand.reshape(-1, right_operand.shape[-1])
    return lax.psum_scatter(
        jnp.einsum("nd,ne->de", left_flat, right_flat, preferred_element_type=jnp.float32).astype(
            jnp.bfloat16
        ),
        "seq",
        scatter_dimension=0,
        tiled=True,
    ).astype(jnp.float32)


def layer_grads(grad_pairs):
    return tuple(
        (spread_rows_out(grad_pairs[index][0], grad_pairs[index][1]) for index in range(4))
    )


def per_device(
    frames_in,
    conditioning,
    mod_first,
    qkv_first,
    out_first,
    up_first,
    down_first,
    mod_second,
    qkv_second,
    out_second,
    up_second,
    down_second,
    cotangent,
):
    clip_count = frames_in.shape[0]
    frame_dev = frames_in.shape[2]
    half_places = frames_in.shape[3]
    features = frames_in.shape[4]
    start_stream = frames_in.reshape(clip_count, frame_dev, half_places, features).astype(
        jnp.float32
    )
    mod_one, mod_two, silu_local, row_start = modulations(conditioning, mod_first, mod_second)
    weights_one = gather_layer(qkv_first, out_first, up_first, down_first)
    spatial_out, unused_one = forward_layer(start_stream, mod_one, weights_one, True)
    weights_two = gather_layer(qkv_second, out_second, up_second, down_second)
    temporal_out, unused_two = forward_layer(to_places(spatial_out), mod_two, weights_two, False)
    block_out = to_frames(temporal_out, frame_dev)
    mod_one, mod_two, silu_local, row_start = modulations(conditioning, mod_first, mod_second)
    again_one = gather_layer_again(qkv_first, out_first, up_first, down_first)
    spatial_again, state_one = forward_layer(start_stream, mod_one, again_one, True)
    again_two = gather_layer_again(qkv_second, out_second, up_second, down_second)
    placed_again = to_places(spatial_again)
    unused_three, state_two = forward_layer(placed_again, mod_two, again_two, False)
    cotangent_sites = to_places(cotangent.reshape(clip_count, frame_dev, half_places, features))
    placed_grad, mod_grad_two, pairs_two = backward_layer(
        cotangent_sites, placed_again, mod_two, again_two, state_two, False
    )
    row_attn = qkv_first.shape[0]
    grads_two = layer_grads(pairs_two)
    spatial_grad = to_frames(placed_grad, frame_dev)
    stream_grad, mod_grad_one, pairs_one = backward_layer(
        spatial_grad, start_stream, mod_one, again_one, state_one, True
    )
    grads_one = layer_grads(pairs_one)
    mod_totals = (
        lax.psum(mod_grad_one.astype(jnp.bfloat16), "seq").astype(jnp.float32),
        lax.psum(mod_grad_two.astype(jnp.bfloat16), "seq").astype(jnp.float32),
    )
    low_one = mod_totals[0].astype(jnp.bfloat16)
    low_two = mod_totals[1].astype(jnp.bfloat16)
    mod_weight_one = jnp.einsum(
        "cd,ce->de", silu_local, low_one, preferred_element_type=jnp.float32
    )
    mod_weight_two = jnp.einsum(
        "cd,ce->de", silu_local, low_two, preferred_element_type=jnp.float32
    )
    silu_grad = jnp.einsum("ce,de->cd", low_one, mod_first, preferred_element_type=jnp.float32)
    silu_grad = silu_grad + jnp.einsum(
        "ce,de->cd", low_two, mod_second, preferred_element_type=jnp.float32
    )
    condition_local = lax.dynamic_slice_in_dim(conditioning, row_start, row_attn, 1)
    condition_grad = jax.vjp(jax.nn.silu, condition_local)[1](silu_grad)[0]
    summed = (
        lax.psum(mod_weight_one.astype(jnp.bfloat16), "rep").astype(jnp.float32),
        lax.psum(grads_one[0].astype(jnp.bfloat16), "rep").astype(jnp.float32),
        lax.psum(grads_one[1].astype(jnp.bfloat16), "rep").astype(jnp.float32),
        lax.psum(grads_one[2].astype(jnp.bfloat16), "rep").astype(jnp.float32),
        lax.psum(grads_one[3].astype(jnp.bfloat16), "rep").astype(jnp.float32),
        lax.psum(mod_weight_two.astype(jnp.bfloat16), "rep").astype(jnp.float32),
        lax.psum(grads_two[0].astype(jnp.bfloat16), "rep").astype(jnp.float32),
        lax.psum(grads_two[1].astype(jnp.bfloat16), "rep").astype(jnp.float32),
        lax.psum(grads_two[2].astype(jnp.bfloat16), "rep").astype(jnp.float32),
        lax.psum(grads_two[3].astype(jnp.bfloat16), "rep").astype(jnp.float32),
    )
    out_shape = (clip_count, 1, frame_dev, half_places, features)
    return (
        block_out.reshape(out_shape),
        stream_grad.reshape(out_shape),
        condition_grad,
        summed[0],
        summed[1],
        summed[2],
        summed[3],
        summed[4],
        summed[5],
        summed[6],
        summed[7],
        summed[8],
        summed[9],
    )


def solution(mesh):
    return jax.shard_map(
        per_device,
        mesh=mesh,
        in_specs=(
            P("rep", "seq", None, None, None),
            P("rep", None),
            P("seq", None),
            P("seq", None),
            P("seq", None),
            P("seq", None),
            P("seq", None),
            P("seq", None),
            P("seq", None),
            P("seq", None),
            P("seq", None),
            P("seq", None),
            P("rep", "seq", None, None, None),
        ),
        out_specs=(
            P("rep", "seq", None, None, None),
            P("rep", "seq", None, None, None),
            P("rep", "seq"),
            P("seq", None),
            P("seq", None),
            P("seq", None),
            P("seq", None),
            P("seq", None),
            P("seq", None),
            P("seq", None),
            P("seq", None),
            P("seq", None),
            P("seq", None),
        ),
        check_vma=False,
    )
```

profile of v0, /device:TPU:0, one launch (start us, length us, event | category | flops | bytes accessed | tf_op | source)
XLA Modules:
  0.0 1629.8 jit_solution(10004412810075176240)
XLA Ops:
  17.6 26.8 %all-reduce = (f32[1,6912]{1,0:T(1,128)S(1)}, f32[1,6912]{1,0:T(1,128)S(1)}) all-reduce(f32[1,6912]{1,0:T(1,128)S(1)} %fusion.149, f32[1,6912]{1,0:T(1,128)S(1)} %fusion.147), channel_id=1, replica_groups=mesh['rep'=4,'seq'=8] {'seq'}, use_global_device_ids=true, to_apply=%region_0.1 | all-reduce | flops 13824 | bytes 110592 | tf_op jit(solution)/shard_map/psum | solution.py:58
  44.6 21.0 %all-gather.9.cloned.1.call-done = bf16[1152,3456]{1,0:T(8,128)(2,1)} async-done(((bf16[144,3456]{1,0:T(8,128)(2,1)}), bf16[1152,3456]{1,0:T(8,128)(2,1)}) %all-gather.9.cloned.1.call-update) | async-done | bytes 7962640 | tf_op jit(solution)/shard_map/all_gather | solution.py:64
  65.6 8.8 fusion.60
  103.3 4.9 fusion.178
  109.1 22.1 %fusion.119 = bf16[4,16,72,128]{3,2,1,0:T(8,128)(2,1)} fusion(bf16[1,4,128,16,72]{2,4,3,1,0:T(8,128)(2,1)} %bitcast.356, bf16[1,4,128,16,72]{2,4,3,1,0:T(8,128)(2,1)} %bitcast.354, f32[4,16,128]{2,1,0:T(8,128)S(1)} %get-tuple-element.81, f32[4,16,128,256]{3,2,1,0:T(8,128)} %copy-done.5), kind=kOutput, calls=%fused_computation.180 | convolution fusion | flops 317792512 | bytes 11960320 | tf_op jit(solution)/shard_map/cshlm,csmhe->cslhe/dot_general | solution.py:142
  131.2 5.5 fusion.173
  138.6 36.5 %all-gather.13.cloned.1.call-done = bf16[1152,4608]{1,0:T(8,128)(2,1)} async-done(((bf16[144,4608]{1,0:T(8,128)(2,1)}), bf16[1152,4608]{1,0:T(8,128)(2,1)}) %all-gather.13.cloned.1.call-update) | async-done | bytes 10616848 | tf_op jit(solution)/shard_map/all_gather | solution.py:66
  175.1 23.9 %fusion.22 = f32[4,128,4608]{2,1,0:T(8,128)} fusion(bf16[1152,4608]{1,0:T(8,128)(2,1)} %all-gather.13.cloned.1.call-done, f32[4,128,1152]{2,1,0:T(8,128)} %copy-done.3, f32[1152]{0:T(1024)S(1)} %get-tuple-element.32, f32[1152]{0:T(1024)S(1)} %get-tuple-element.33, f32[4,128]{1,0:T(4,128)S(1)} %fusion.144, f32[4,128]{1,0:T(4,128)S(1)} %broadcast_multiply_fusion.2), kind=kOutput, calls=%fused_computation.32 | convolution fusion | flops 5438767104 | bytes 22426624 | tf_op jit(solution)/shard_map/csld,de->csle/dot_general | solution.py:37
  199.1 41.6 %all-gather.15.cloned.1.call-done = bf16[4608,1152]{1,0:T(8,128)(2,1)} async-done(((bf16[576,1152]{1,0:T(8,128)(2,1)}), bf16[4608,1152]{1,0:T(8,128)(2,1)}) %all-gather.15.cloned.1.call-update) | async-done | bytes 10616848 | tf_op jit(solution)/shard_map/all_gather | solution.py:67
  240.7 13.8 add_convert_fusion.4
  268.2 9.0 all-to-all-done
  290.9 9.5 all-gather.17.cloned.1.call-done
  300.4 9.0 fusion.57
  311.1 5.7 reshape.1276
  316.8 5.8 reshape.1277
  322.6 4.8 reshape.1275
  330.9 16.3 %fusion.179 = (f32[32,16,16]{2,1,0:T(8,128)S(1)}, f32[32,16,16,16]{2,3,1,0:T(8,128)S(1)}) fusion(f32[32,16,16,16]{2,3,1,0:T(8,128)S(1)} %fusion.109), kind=kOutput, calls=%fused_computation.279 | output fusion | flops 524303 | bytes 1081344 | tf_op jit(solution)/shard_map/sub | solution.py:139
  355.0 6.6 fusion.172
  363.9 34.0 %all-gather.21.cloned.1.call-done = bf16[1152,4608]{1,0:T(8,128)(2,1)} async-done(((bf16[144,4608]{1,0:T(8,128)(2,1)}), bf16[1152,4608]{1,0:T(8,128)(2,1)}) %all-gather.21.cloned.1.call-update) | async-done | bytes 10616848 | tf_op jit(solution)/shard_map/all_gather | solution.py:66
  397.9 13.2 fusion.14
  411.1 52.6 %all-gather.23.cloned.1.call-done = bf16[4608,1152]{1,0:T(8,128)(2,1)} async-done(((bf16[576,1152]{1,0:T(8,128)(2,1)}), bf16[4608,1152]{1,0:T(8,128)(2,1)}) %all-gather.23.cloned.1.call-update) | async-done | bytes 10616848 | tf_op jit(solution)/shard_map/all_gather | solution.py:67
  463.7 16.0 fusion.37
  479.6 13.5 multiply_reduce_fusion.13
  497.5 18.1 %multiply_reduce_fusion.4 = (bf16[1152]{0:T(1024)(128)(2,1)}, bf16[32,16,1152]{2,1,0:T(8,128)(2,1)}, bf16[1152]{0:T(1024)(128)(2,1)}, f32[32,16,1152]{2,1,0:T(8,128)S(1)}) fusion(f32[32,16,1152]{2,1,0:T(8,128)} %reshape.1279, f32[32,16,1152]{2,1,0:T(8,128)} %get-tuple-element.59, f32[1152]{0:T(1024)S(1)} %get-tuple-element.25, ...), kind=kOutput, calls=%fused_computation.133 | convolution fusion | flops 5465896960 | bytes 33052160 | tf_op jit(solution)/shard_map/csld,de->csle/dot_general | solution.py:37
  520.2 4.7 reshape.1280
  563.1 10.9 multiply_reduce_fusion.12
  597.4 4.9 convolution_convert_fusion
  606.5 17.4 %fusion.30 = bf16[4,128,4608]{2,1,0:T(8,128)(2,1)} fusion(f32[4,128,4608]{2,1,0:T(8,128)} %fusion.22, bf16[4608,1152]{1,0:T(8,128)(2,1)} %all-gather.15.cloned.1.call-done, f32[4,128,1152]{2,1,0:T(8,128)S(1)} %bitcast.337, f32[1152]{0:T(1024)S(1)} %copy-done.64), kind=kOutput, calls=%fused_computation.40 | convolution fusion | flops 5484183552 | bytes 27136512 | tf_op jit(solution)/shard_map/csle,de->csld/dot_general | solution.py:43
  624.0 11.9 multiply_reduce_fusion.11
  646.3 10.6 fusion.7
  657.0 4.7 convolution_convert_fusion.2
  664.3 22.2 %convolution_bitcast_fusion.6 = f32[1,4,256,16,72]{2,4,3,1,0:T(8,128)} fusion(bf16[4,128,16,72]{1,3,2,0:T(8,128)(2,1)} %bitcast.360, f32[4,16,128]{2,1,0:T(8,128)S(1)} %copy-done.54, f32[4,16,128,256]{3,2,1,0:T(8,128)} %copy-done.5), kind=kOutput, calls=%fused_computation.161 | convolution fusion | flops 312484096 | bytes 14319616 | tf_op jit(solution)/shard_map/cshlm,cslhe->csmhe/dot_general | solution.py:219
  686.5 7.5 multiply_reduce_fusion
  710.4 5.2 fusion.92
  721.0 9.8 fusion.6
  732.1 13.0 fusion.3
  745.8 11.2 fusion.2
  758.5 12.1 fusion.5
  771.3 11.5 fusion.4
  784.2 10.9 fusion.85
  797.8 23.5 %all-reduce.1 = (bf16[6912]{0:T(1024)(128)(2,1)S(1)}, bf16[6912]{0:T(1024)(128)(2,1)S(1)}) all-reduce(bf16[6912]{0:T(1024)(128)(2,1)S(1)} %reduce.79, bf16[6912]{0:T(1024)(128)(2,1)S(1)} %reduce.80), channel_id=1, replica_groups=mesh['rep'=4,'seq'=8] {'seq'}, use_global_device_ids=true, to_apply=%region_30.31 | all-reduce | flops 13824 | bytes 55296 | tf_op jit(solution)/shard_map/psum | solution.py:326
  823.8 20.3 %reduce-scatter.9.cloned.1.call-done = bf16[144,3456]{1,0:T(8,128)(2,1)} async-done(((bf16[1152,3456]{1,0:T(8,128)(2,1)}), bf16[144,3456]{1,0:T(8,128)(2,1)}) %reduce-scatter.9.cloned.1.call-update) | async-done | bytes 995344 | tf_op jit(solution)/shard_map/reduce_scatter | solution.py:264
  844.1 85.7 %reduce-scatter.23.cloned.1.call-done = bf16[576,1152]{1,0:T(8,128)(2,1)} async-done(((bf16[4608,1152]{1,0:T(8,128)(2,1)}), bf16[576,1152]{1,0:T(8,128)(2,1)}) %reduce-scatter.23.cloned.1.call-update) | async-done | bytes 1327120 | tf_op jit(solution)/shard_map/reduce_scatter | solution.py:264
  929.8 85.6 %reduce-scatter.21.cloned.1.call-done = bf16[144,4608]{1,0:T(8,128)(2,1)} async-done(((bf16[1152,4608]{1,0:T(8,128)(2,1)}), bf16[144,4608]{1,0:T(8,128)(2,1)}) %reduce-scatter.21.cloned.1.call-update) | async-done | bytes 1327120 | tf_op jit(solution)/shard_map/reduce_scatter | solution.py:264
  1015.4 85.6 %reduce-scatter.15.cloned.1.call-done = bf16[576,1152]{1,0:T(8,128)(2,1)} async-done(((bf16[4608,1152]{1,0:T(8,128)(2,1)}), bf16[576,1152]{1,0:T(8,128)(2,1)}) %reduce-scatter.15.cloned.1.call-update) | async-done | bytes 1327120 | tf_op jit(solution)/shard_map/reduce_scatter | solution.py:264
  1101.0 85.6 %reduce-scatter.13.cloned.1.call-done = bf16[144,4608]{1,0:T(8,128)(2,1)} async-done(((bf16[1152,4608]{1,0:T(8,128)(2,1)}), bf16[144,4608]{1,0:T(8,128)(2,1)}) %reduce-scatter.13.cloned.1.call-update) | async-done | bytes 1327120 | tf_op jit(solution)/shard_map/reduce_scatter | solution.py:264
  1191.4 19.3 %all_to_all.16 = bf16[8,1,4,1,16,1152]{5,4,2,3,1,0:T(8,128)(2,1)S(1)} all-to-all(bf16[8,1,4,1,16,1152]{5,4,2,3,1,0:T(8,128)(2,1)S(1)} %bitcast.348), channel_id=1, replica_groups=mesh['rep'=4,'seq'=8] {'seq'}, dimensions={0} | all-to-all | bytes 2359296 | tf_op jit(solution)/shard_map/all_to_all | solution.py:114
  1217.3 386.7 %all-reduce.5.cloned.1.call-done = (bf16[144,6912]{1,0:T(8,128)(2,1)}, bf16[144,3456]{1,0:T(8,128)(2,1)}, bf16[144,1152]{1,0:T(8,128)(2,1)}, bf16[144,4608]{1,0:...) async-done(((bf16[144,6912]{1,0:T(8,128)(2,1)}, ...) | async-done | bytes 11943952 | tf_op jit(solution)/shard_map/psum | solution.py:344
  (419 shorter events, 234.6 us)
Async XLA Ops:
  7.2 58.4 %all-gather.9.cloned.1.call-start = ((), (), s32[]{:S(2)}) async-start(), calls=%async_computation.12 | async-start | bytes 8957952 | tf_op jit(solution)/shard_map/all_gather | solution.py:64
  7.9 123.3 %all-gather.11.cloned.1.call-start = ((), (), s32[]{:S(2)}) async-start(), calls=%async_computation.13 | async-start | bytes 2985984 | tf_op jit(solution)/shard_map/all_gather | solution.py:65
  8.7 166.4 %all-gather.13.cloned.1.call-start = ((), (), s32[]{:S(2)}) async-start(), calls=%async_computation.14 | async-start | bytes 11943936 | tf_op jit(solution)/shard_map/all_gather | solution.py:66
  9.4 231.3 %all-gather.15.cloned.1.call-start = ((), (), s32[]{:S(2)}) async-start(), calls=%async_computation.15 | async-start | bytes 11943936 | tf_op jit(solution)/shard_map/all_gather | solution.py:67
  10.0 290.4 %all-gather.17.cloned.1.call-start = ((), (), s32[]{:S(2)}) async-start(), calls=%async_computation.16 | async-start | bytes 8957952 | tf_op jit(solution)/shard_map/all_gather | solution.py:64
  10.6 344.4 %all-gather.19.cloned.1.call-start = ((), (), s32[]{:S(2)}) async-start(), calls=%async_computation.17 | async-start | bytes 2985984 | tf_op jit(solution)/shard_map/all_gather | solution.py:65
  11.2 386.8 %all-gather.21.cloned.1.call-start = ((), (), s32[]{:S(2)}) async-start(), calls=%async_computation.18 | async-start | bytes 11943936 | tf_op jit(solution)/shard_map/all_gather | solution.py:66
  11.9 451.7 %all-gather.23.cloned.1.call-start = ((), (), s32[]{:S(2)}) async-start(), calls=%async_computation.19 | async-start | bytes 11943936 | tf_op jit(solution)/shard_map/all_gather | solution.py:67
  12.9 52.7 %copy-start.70 = (f32[4,128]{1,0:T(4,128)}, f32[4,128]{1,0:T(4,128)S(1)}, u32[]{:S(2)}) copy-start(f32[4,128]{1,0:T(4,128)S(1)} %broadcast_multiply_fusion.3) | copy-start | bytes 6148
  13.4 61.0 %copy-start.80 = (f32[4,128]{1,0:T(4,128)}, f32[4,128]{1,0:T(4,128)S(1)}, u32[]{:S(2)}) copy-start(f32[4,128]{1,0:T(4,128)S(1)} %fusion.143) | copy-start | bytes 6148
  44.5 29.9 %copy-start.58 = (f32[1152]{0:T(1024)}, f32[1152]{0:T(1024)S(1)}, u32[]{:S(2)}) copy-start(f32[1152]{0:T(1024)S(1)} %get-tuple-element.35) | copy-start | bytes 13828
  44.5 29.9 %copy-start.96 = (f32[1152]{0:T(1024)}, f32[1152]{0:T(1024)S(1)}, u32[]{:S(2)}) copy-start(f32[1152]{0:T(1024)S(1)} %get-tuple-element.34) | copy-start | bytes 13828
  44.6 86.6 %copy-start.49 = (f32[1152]{0:T(1024)}, f32[1152]{0:T(1024)S(1)}, u32[]{:S(2)}) copy-start(f32[1152]{0:T(1024)S(1)} %get-tuple-element.36) | copy-start | bytes 13828
  44.6 130.5 %copy-start.55 = (f32[1152]{0:T(1024)}, f32[1152]{0:T(1024)S(1)}, u32[]{:S(2)}) copy-start(f32[1152]{0:T(1024)S(1)} %get-tuple-element.33) | copy-start | bytes 13828
  44.6 130.5 %copy-start.94 = (f32[1152]{0:T(1024)}, f32[1152]{0:T(1024)S(1)}, u32[]{:S(2)}) copy-start(f32[1152]{0:T(1024)S(1)} %get-tuple-element.32) | copy-start | bytes 13828
  44.6 196.1 %copy-start.63 = (f32[1152]{0:T(1024)}, f32[1152]{0:T(1024)S(1)}, u32[]{:S(2)}) copy-start(f32[1152]{0:T(1024)S(1)} %get-tuple-element.31) | copy-start | bytes 13828
  78.1 13.9 collective-permute-start
  80.2 175.4 %all-to-all-start.2 = ((bf16[1,1,4,8,16,1152]{5,4,2,1,0,3:T(8,128)(2,1)}), bf16[1,1,4,8,16,1152]{5,4,2,1,0,3:T(8,128)(2,1)}, u32[]{:S(2)}, u32[]{:S(2)}) async-start(bf16[1,1,4,8,16,1152]{5,4,2,1,0,3:T(8,128)(2,1)} %copy.281), calls=%async_computation.2 | async-start | bytes 2359296 | tf_op jit(solution)/shard_map/all_to_all | solution.py:92
  109.1 22.1 %copy-start.53 = (f32[4,16,128]{2,1,0:T(8,128)}, f32[4,16,128]{2,1,0:T(8,128)S(1)}, u32[]{:S(2)}) copy-start(f32[4,16,128]{2,1,0:T(8,128)S(1)} %get-tuple-element.81) | copy-start | bytes 98308
  136.8 62.3 %copy-start.73 = (f32[4,128]{1,0:T(4,128)}, f32[4,128]{1,0:T(4,128)S(1)}, u32[]{:S(2)}) copy-start(f32[4,128]{1,0:T(4,128)S(1)} %broadcast_multiply_fusion.2) | copy-start | bytes 6148
  138.5 60.5 %copy-start.78 = (f32[4,128]{1,0:T(4,128)}, f32[4,128]{1,0:T(4,128)S(1)}, u32[]{:S(2)}) copy-start(f32[4,128]{1,0:T(4,128)S(1)} %multiply_reduce_fusion.16) | copy-start | bytes 6148
  138.5 60.5 %copy-start.83 = (f32[4,128]{1,0:T(4,128)}, f32[4,128]{1,0:T(4,128)S(1)}, u32[]{:S(2)}) copy-start(f32[4,128]{1,0:T(4,128)S(1)} %fusion.144) | copy-start | bytes 6148
  255.6 21.5 %all-to-all-start = ((bf16[1,1,4,8,16,1152]{5,4,2,1,0,3:T(8,128)(2,1)}), bf16[1,1,4,8,16,1152]{5,4,2,1,0,3:T(8,128)(2,1)S(1)}, u32[]{:S(2)}, u32[]{:S(2)}) async-start(bf16[1,1,4,8,16,1152]{5,4,2,1,0,3:T(8,128)(2,1)} %copy.260), calls=%async_computation | async-start | bytes 2359296 | tf_op jit(solution)/shard_map/all_to_all | solution.py:92
  259.3 41.2 %copy-start.100 = (f32[1152]{0:T(1024)}, f32[1152]{0:T(1024)S(1)}, u32[]{:S(2)}) copy-start(f32[1152]{0:T(1024)S(1)} %get-tuple-element.28) | copy-start | bytes 13828
  259.3 138.6 %copy-start.98 = (f32[1152]{0:T(1024)}, f32[1152]{0:T(1024)S(1)}, u32[]{:S(2)}) copy-start(f32[1152]{0:T(1024)S(1)} %get-tuple-element.26) | copy-start | bytes 13828
  259.3 238.2 %copy-start.66 = (f32[1152]{0:T(1024)}, f32[1152]{0:T(1024)S(1)}, u32[]{:S(2)}) copy-start(f32[1152]{0:T(1024)S(1)} %get-tuple-element.27) | copy-start | bytes 13828
  259.3 238.2 %copy-start.68 = (f32[1152]{0:T(1024)}, f32[1152]{0:T(1024)S(1)}, u32[]{:S(2)}) copy-start(f32[1152]{0:T(1024)S(1)} %get-tuple-element.25) | copy-start | bytes 13828
  330.9 16.4 %copy-start.33 = (bf16[32,16,16,72]{3,2,1,0:T(8,128)(2,1)S(1)}, bf16[32,16,16,72]{3,2,1,0:T(8,128)(2,1)}, u32[]{:S(2)}) copy-start(bf16[32,16,16,72]{3,2,1,0:T(8,128)(2,1)} %reshape.1275) | copy-start | bytes 3538948
  361.7 135.8 %copy-start.51 = (f32[32,16]{1,0:T(8,128)}, f32[32,16]{1,0:T(8,128)S(1)}, u32[]{:S(2)}) copy-start(f32[32,16]{1,0:T(8,128)S(1)} %copy.275) | copy-start | bytes 6148
  363.9 133.6 %copy-start.61 = (f32[32,16]{1,0:T(8,128)}, f32[32,16]{1,0:T(8,128)S(1)}, u32[]{:S(2)}) copy-start(f32[32,16]{1,0:T(8,128)S(1)} %copy.277) | copy-start | bytes 6148
  463.7 16.0 copy-start.11
  479.6 13.5 copy-start.106
  586.0 20.3 %all-to-all-start.3 = ((bf16[8,1,4,1,16,1152]{5,4,2,3,1,0:T(8,128)(2,1)}), bf16[8,1,4,1,16,1152]{5,4,2,3,1,0:T(8,128)(2,1)S(1)}, u32[]{:S(2)}, u32[]{:S(2)}) async-start(bf16[8,1,4,1,16,1152]{5,4,2,3,1,0:T(8,128)(2,1)} %bitcast.346), calls=%async_computation.3 | async-start | bytes 2359296 | tf_op jit(solution)/shard_map/all_to_all | solution.py:114
  589.5 234.3 %reduce-scatter.19.cloned.1.call-start = ((), (), s32[]{:S(2)}) async-start(), calls=%async_computation.25 | async-start | bytes 2985984 | tf_op jit(solution)/shard_map/reduce_scatter | solution.py:264
  602.3 221.5 %reduce-scatter.11.cloned.1.call-start = ((), (), s32[]{:S(2)}) async-start(), calls=%async_computation.21 | async-start | bytes 2985984 | tf_op jit(solution)/shard_map/reduce_scatter | solution.py:264
  606.3 17.7 %copy-start.20 = (bf16[8,1,4,1,16,1152]{5,4,2,3,1,0:T(8,128)(2,1)}, bf16[8,1,4,1,16,1152]{5,4,2,3,1,0:T(8,128)(2,1)S(1)}, u32[]{:S(2)}) copy-start(bf16[8,1,4,1,16,1152]{5,4,2,3,1,0:T(8,128)(2,1)S(1)} %all-to-all-done.3) | copy-start | bytes 3538948
  606.5 17.5 %copy-start.4 = (f32[4,128,1152]{2,1,0:T(8,128)S(1)}, f32[4,128,1152]{2,1,0:T(8,128)}, u32[]{:S(2)}) copy-start(f32[4,128,1152]{2,1,0:T(8,128)} %copy-done.3) | copy-start | bytes 7077892
  606.5 17.5 %copy-start.56 = (f32[1152]{0:T(1024)S(1)}, f32[1152]{0:T(1024)}, u32[]{:S(2)}) copy-start(f32[1152]{0:T(1024)} %copy-done.55) | copy-start | bytes 13828
  606.5 17.5 %copy-start.74 = (f32[4,128]{1,0:T(4,128)S(1)}, f32[4,128]{1,0:T(4,128)}, u32[]{:S(2)}) copy-start(f32[4,128]{1,0:T(4,128)} %copy-done.73) | copy-start | bytes 6148
  645.7 178.1 %reduce-scatter.17.cloned.1.call-start = ((), (), s32[]{:S(2)}) async-start(), calls=%async_computation.24 | async-start | bytes 8957952 | tf_op jit(solution)/shard_map/reduce_scatter | solution.py:264
  657.0 187.1 %reduce-scatter.9.cloned.1.call-start = ((), (), s32[]{:S(2)}) async-start(), calls=%async_computation.20 | async-start | bytes 8957952 | tf_op jit(solution)/shard_map/reduce_scatter | solution.py:264
  664.3 22.2 %copy-start.43 = (bf16[1,4,128,1152]{2,3,1,0:T(8,128)(2,1)S(1)}, bf16[1,4,128,1152]{2,3,1,0:T(8,128)(2,1)}, u32[]{:S(2)}) copy-start(bf16[1,4,128,1152]{2,3,1,0:T(8,128)(2,1)} %copy.254) | copy-start | bytes 3538948
  703.0 5.3 collective-permute-start.1
  730.9 199.0 %reduce-scatter.23.cloned.1.call-start = ((), (), s32[]{:S(2)}) async-start(), calls=%async_computation.27 | async-start | bytes 11943936 | tf_op jit(solution)/shard_map/reduce_scatter | solution.py:264
  745.1 270.3 %reduce-scatter.21.cloned.1.call-start = ((), (), s32[]{:S(2)}) async-start(), calls=%async_computation.26 | async-start | bytes 11943936 | tf_op jit(solution)/shard_map/reduce_scatter | solution.py:264
  757.0 344.0 %reduce-scatter.15.cloned.1.call-start = ((), (), s32[]{:S(2)}) async-start(), calls=%async_computation.23 | async-start | bytes 11943936 | tf_op jit(solution)/shard_map/reduce_scatter | solution.py:264
  770.6 416.0 %reduce-scatter.13.cloned.1.call-start = ((), (), s32[]{:S(2)}) async-start(), calls=%async_computation.22 | async-start | bytes 11943936 | tf_op jit(solution)/shard_map/reduce_scatter | solution.py:264
  782.9 821.1 %all-reduce.5.cloned.1.call-start = ((), (), s32[]{:S(2)}) async-start(), calls=%async_computation.28 | async-start | bytes 23887872 | tf_op jit(solution)/shard_map/psum | solution.py:344
  (83 other events, 250.4 us)
Sparse Core Ops, SparseCore 0:
  9.9 55.5 all-gather.8
  67.4 38.6 all-gather.10
  108.1 66.9 all-gather.12
  176.8 63.8 all-gather.14
  242.4 57.9 all-gather.16
  302.2 29.9 all-gather.18
  334.1 63.8 all-gather.20
  399.8 63.8 all-gather.22
  602.4 45.0 reduce-scatter.18
  651.8 43.7 reduce-scatter.10
  699.2 70.5 reduce-scatter.16
  773.5 70.5 reduce-scatter.8
  847.6 82.1 reduce-scatter.22
  933.2 82.2 reduce-scatter.20
  1018.8 82.2 reduce-scatter.14
  1104.4 82.2 reduce-scatter.12
  1191.6 412.4 all-reduce.4
where the time goes:
time: 1640 us; the launch traced here: 1630 us
  waiting for transfers between devices  963 us (59%)
  matrix products  338 us (21%)
  local copies, waits for them, and re-layouts  141 us (9%)
  other arithmetic  90 us (5%)
  blocking collectives  69.6 us (4%)
    psum x1, waiting for transfers between devices, per_device(): lax.psum(mod_weight_one.astype(jnp.bfloat16), 'rep').astype(jnp.float32)  387 us
    reduce_scatter x8, waiting for transfers between devices, spread_rows_out(): lax.psum_scatter(jnp.einsum('nd,ne->de', left_flat, right_flat, preferred...  363 us
    dot_general x8, matrix products, project(): jnp.einsum('csld,de->csle', left_operand, right_operand, preferred_elemen...  99 us
    all_gather x2, waiting for transfers between devices, gather_layer(): lax.all_gather(down_w, 'seq', axis=0, tiled=True)  94.2 us
    dot_general x8, matrix products, project_back(): jnp.einsum('csle,de->csld', incoming, right_operand, preferred_element_ty...  87.1 us
    dot_general x8, matrix products, spread_rows_out(): jnp.einsum('nd,ne->de', left_flat, right_flat, preferred_element_type=jnp...  76.2 us
    all_gather x2, waiting for transfers between devices, gather_layer(): lax.all_gather(up_w, 'seq', axis=0, tiled=True)  70.6 us
  transfers between devices with their start and end apart: 22, of which 14 were waited for; matrix products, arithmetic and copies ran while one was open for 25% of the time, Pallas kernels for 0%

commit v1 on v0

--- a/solution.py
+++ b/solution.py
@@ -6,6 +6,22 @@
 HEADS = 16
 HEAD_WIDTH = 72
 norm_epsilon = 1e-06
+
+
+def collect(x, axis, dim):
+    ways, here, lap = (lax.axis_size(axis), lax.axis_index(axis), x.shape[dim])
+    shape = [n * ways if d == dim else n for d, n in enumerate(x.shape)]
+    full = lax.dynamic_update_slice_in_dim(jnp.zeros(shape, x.dtype), x, here * lap, axis=dim)
+    going_up = going_down = x
+    for far in range(1, ways // 2 + 1):
+        going_up = lax.ppermute(going_up, axis, [(d, (d + 1) % ways) for d in range(ways)])
+        full = lax.dynamic_update_slice_in_dim(full, going_up, (here - far) % ways * lap, axis=dim)
+        if 2 * far < ways:
+            going_down = lax.ppermute(going_down, axis, [(d, (d - 1) % ways) for d in range(ways)])
+            full = lax.dynamic_update_slice_in_dim(
+                full, going_down, (here + far) % ways * lap, axis=dim
+            )
+    return full
 
 
 def from_partner(block, axis, apart):
@@ -64,7 +80,7 @@
         lax.all_gather(qkv_w, "seq", axis=0, tiled=True),
         lax.all_gather(out_w, "seq", axis=0, tiled=True),
         lax.all_gather(up_w, "seq", axis=0, tiled=True),
-        lax.all_gather(down_w, "seq", axis=0, tiled=True),
+        collect(down_w, "seq", 0),
     )
 
 

time: 1640 us -> 1720 us (1.049)
  waiting for transfers between devices: 963 us -> 861 us
  local copies, waits for them, and re-layouts: 141 us -> 207 us
  blocking collectives: 69.6 us -> 112 us
  matrix products: 338 us -> 376 us
  starting transfers between devices: 13.1 us -> 34 us
    ppermute x0 -> x14, waiting for transfers between devices: none -> 202 us  [the longest x8 139 us: collect(): lax.ppermute(going_up, axis, [(d, (d + 1) % ways) for d in range(ways)])]
    reduce_scatter x8, waiting for transfers between devices: 363 us -> 258 us  [spread_rows_out(): lax.psum_scatter(jnp.einsum('nd,ne->de', left_flat, right_flat, preferred...]
    psum x1, waiting for transfers between devices: 387 us -> 289 us  [per_device(): lax.psum(mod_weight_one.astype(jnp.bfloat16), 'rep').astype(jnp.float32)]
    all_gather x2, waiting for transfers between devices: 70.6 us -> 24.4 us  [gather_layer(): lax.all_gather(up_w, 'seq', axis=0, tiled=True)]
    all_gather x2, waiting for transfers between devices: 94.2 us -> 55.7 us  [gather_layer_again(): lax.all_gather(down_w, 'seq', axis=0, tiled=True)]
    psum x1, blocking collectives: 26.8 us -> 64.6 us  [modulations(): summed = lax.psum((part_one, part_two), 'seq')]
    dot_general x8 -> x12, matrix products: 99 us -> 136 us  [project(): jnp.einsum('csld,de->csle', left_operand, right_operand, preferred_elemen...]
    all_gather x2, waiting for transfers between devices: 30.5 us -> 0.01 us  [gather_layer(): lax.all_gather(qkv_w, 'seq', axis=0, tiled=True)]
  transfers between devices with their start and end apart: 22 -> 37, of which waited for: 14 -> 20; matrix products, arithmetic and copies ran while one was open for 25% -> 32% of each run, Pallas kernels for 0% -> 0%
where the time goes in v1:
time: 1720 us; the launch traced here: 1710 us
  waiting for transfers between devices  861 us (50%)
  matrix products  376 us (22%)
  local copies, waits for them, and re-layouts  207 us (12%)
  blocking collectives  112 us (7%)
  other arithmetic  107 us (6%)
  starting transfers between devices  34 us (2%)
    psum x1, waiting for transfers between devices, per_device(): lax.psum(mod_weight_one.astype(jnp.bfloat16), 'rep').astype(jnp.float32)  289 us
    reduce_scatter x8, waiting for transfers between devices, spread_rows_out(): lax.psum_scatter(jnp.einsum('nd,ne->de', left_flat, right_flat, preferred...  258 us
    ppermute x8, waiting for transfers between devices, collect(): lax.ppermute(going_up, axis, [(d, (d + 1) % ways) for d in range(ways)])  139 us
    dot_general x12, matrix products, project(): jnp.einsum('csld,de->csle', left_operand, right_operand, preferred_elemen...  136 us
    dot_general x8, matrix products, project_back(): jnp.einsum('csle,de->csld', incoming, right_operand, preferred_element_ty...  82.6 us
    dot_general x8, matrix products, spread_rows_out(): jnp.einsum('nd,ne->de', left_flat, right_flat, preferred_element_type=jnp...  76.7 us
    psum x1, blocking collectives, modulations(): summed = lax.psum((part_one, part_two), 'seq')  64.6 us
    ppermute x6, waiting for transfers between devices, collect(): lax.ppermute(going_down, axis, [(d, (d - 1) % ways) for d in range(ways)])  62.8 us
  transfers between devices with their start and end apart: 37, of which 20 were waited for; matrix products, arithmetic and copies ran while one was open for 32% of the time, Pallas kernels for 0%

profile of v1, /device:TPU:0, one launch (start us, length us, event | category | flops | bytes accessed | tf_op | source)
XLA Modules:
  0.0 1712.8 jit_solution(18153917742954372537)
XLA Ops:
  25.3 28.0 %collective-permute-done.1 = bf16[576,1152]{1,0:T(8,128)(2,1)} collective-permute-done((bf16[576,1152]{1,0:T(8,128)(2,1)}, bf16[576,1152]{1,0:T(8,128)(2,1)}, u32[]{:S(2)}, u32[]{:S(2)}) %collective-permute-start.1) | collective-permute-done | bytes 1327136 | tf_op jit(solution)/shard_map/ppermute | solution.py:17
  57.2 64.6 %all-reduce = (f32[1,6912]{1,0:T(1,128)S(1)}, f32[1,6912]{1,0:T(1,128)S(1)}) all-reduce(f32[1,6912]{1,0:T(1,128)S(1)} %fusion.226, f32[1,6912]{1,0:T(1,128)S(1)} %fusion.224), channel_id=1, replica_groups=mesh['rep'=4,'seq'=8] {'seq'}, use_global_device_ids=true, to_apply=%region_0.1 | all-reduce | flops 13824 | bytes 110592 | tf_op jit(solution)/shard_map/psum | solution.py:74
  123.6 8.9 fusion.85
  144.2 22.3 %collective-permute-done.4 = bf16[576,1152]{1,0:T(8,128)(2,1)} collective-permute-done((bf16[576,1152]{1,0:T(8,128)(2,1)}, bf16[576,1152]{1,0:T(8,128)(2,1)}, u32[]{:S(2)}, u32[]{:S(2)}) %collective-permute-start.4) | collective-permute-done | bytes 1327136 | tf_op jit(solution)/shard_map/ppermute | solution.py:20
  182.4 37.5 %collective-permute-done.6 = bf16[576,1152]{1,0:T(8,128)(2,1)S(1)} collective-permute-done((bf16[576,1152]{1,0:T(8,128)(2,1)}, bf16[576,1152]{1,0:T(8,128)(2,1)S(1)}, u32[]{:S(2)}, u32[]{:S(2)}) %collective-permute-start.6) | collective-permute-done | bytes 1327136 | tf_op jit(solution)/shard_map/ppermute | solution.py:20
  251.4 21.9 %fusion.181 = bf16[4,16,72,128]{3,2,1,0:T(8,128)(2,1)} fusion(bf16[1,4,128,16,72]{2,4,3,1,0:T(8,128)(2,1)} %bitcast.429, bf16[1,4,128,16,72]{2,4,3,1,0:T(8,128)(2,1)} %bitcast.427, f32[4,16,128]{2,1,0:T(8,128)S(1)} %get-tuple-element.80, f32[4,16,128,256]{3,2,1,0:T(8,128)} %copy-done.10), kind=kOutput, calls=%fused_computation.225 | convolution fusion | flops 317792512 | bytes 11960320 | tf_op jit(solution)/shard_map/cshlm,csmhe->cslhe/dot_general | solution.py:158
  273.3 5.7 fusion.256
  280.9 12.8 fusion.29
  296.9 13.8 add_convert_fusion.3
  315.4 12.9 fusion.116
  350.5 17.0 all-to-all-done
  378.8 9.0 fusion.79
  389.5 5.8 reshape.1455
  395.3 5.9 reshape.1457
  409.3 16.3 fusion.265
  433.3 7.3 fusion.255
  442.4 24.3 %all-gather.19.cloned.1.call-done = bf16[1152,4608]{1,0:T(8,128)(2,1)} async-done(((bf16[144,4608]{1,0:T(8,128)(2,1)}), bf16[1152,4608]{1,0:T(8,128)(2,1)}) %all-gather.19.cloned.1.call-update) | async-done | bytes 10616848 | tf_op jit(solution)/shard_map/all_gather | solution.py:82
  466.8 13.2 fusion.21
  479.9 52.6 %all-gather.21.cloned.1.call-done = bf16[4608,1152]{1,0:T(8,128)(2,1)} async-done(((bf16[576,1152]{1,0:T(8,128)(2,1)}), bf16[4608,1152]{1,0:T(8,128)(2,1)}) %all-gather.21.cloned.1.call-update) | async-done | bytes 10616848 | tf_op jit(solution)/shard_map/all_gather | solution.py:92
  532.5 15.9 fusion.44
  548.4 12.2 multiply_reduce_fusion.13
  611.9 9.4 multiply_reduce_fusion.12
  648.1 17.4 %fusion.37 = bf16[4,128,4608]{2,1,0:T(8,128)(2,1)} fusion(f32[4,128,4608]{2,1,0:T(8,128)} %fusion.29, bf16[4608,1152]{1,0:T(8,128)(2,1)} %all-gather.23.cloned.1.call-done, f32[4,128,1152]{2,1,0:T(8,128)S(1)} %bitcast.410, f32[1152]{0:T(1024)S(1)} %copy-done.86), kind=kOutput, calls=%fused_computation.48 | convolution fusion | flops 5484183552 | bytes 27136512 | tf_op jit(solution)/shard_map/csle,de->csld/dot_general | solution.py:59
  665.5 11.9 multiply_reduce_fusion.11
  687.9 10.5 fusion.8
  705.1 21.8 %convolution_bitcast_fusion.6 = f32[1,4,256,16,72]{2,4,3,1,0:T(8,128)} fusion(bf16[4,128,16,72]{1,3,2,0:T(8,128)(2,1)S(1)} %bitcast.432, f32[4,16,128]{2,1,0:T(8,128)S(1)} %copy-done.68, f32[4,16,128,256]{3,2,1,0:T(8,128)} %copy-done.10), kind=kOutput, calls=%fused_computation.198 | convolution fusion | flops 312484096 | bytes 14319616 | tf_op jit(solution)/shard_map/cshlm,cslhe->csmhe/dot_general | solution.py:235
  729.2 6.9 multiply_reduce_fusion
  761.3 9.8 fusion.7
  771.8 11.4 fusion.3
  785.9 13.3 fusion.4
  799.9 11.0 fusion.5
  812.4 12.6 fusion.6
  829.3 43.5 %collective-permute-done.8 = bf16[576,1152]{1,0:T(8,128)(2,1)S(1)} collective-permute-done((bf16[576,1152]{1,0:T(8,128)(2,1)S(1)}, bf16[576,1152]{1,0:T(8,128)(2,1)S(1)}, u32[]{:S(2)}, u32[]{:S(2)}) %collective-permute-start.8) | collective-permute-done | bytes 1327136 | tf_op jit(solution)/shard_map/ppermute | solution.py:17
  878.8 39.4 %collective-permute-done.10 = bf16[576,1152]{1,0:T(8,128)(2,1)} collective-permute-done((bf16[576,1152]{1,0:T(8,128)(2,1)S(1)}, bf16[576,1152]{1,0:T(8,128)(2,1)}, u32[]{:S(2)}, u32[]{:S(2)}) %collective-permute-start.10) | collective-permute-done | bytes 1327136 | tf_op jit(solution)/shard_map/ppermute | solution.py:17
  927.3 23.7 %collective-permute-done.12 = bf16[576,1152]{1,0:T(8,128)(2,1)} collective-permute-done((bf16[576,1152]{1,0:T(8,128)(2,1)}, bf16[576,1152]{1,0:T(8,128)(2,1)}, u32[]{:S(2)}, u32[]{:S(2)}) %collective-permute-start.12) | collective-permute-done | bytes 1327136 | tf_op jit(solution)/shard_map/ppermute | solution.py:17
  952.9 16.6 fusion.185
  969.6 9.3 fusion.138
  981.7 28.0 %all-reduce.1 = (bf16[6912]{0:T(1024)(128)(2,1)S(1)}, bf16[6912]{0:T(1024)(128)(2,1)S(1)}) all-reduce(bf16[6912]{0:T(1024)(128)(2,1)S(1)} %reduce.91, bf16[6912]{0:T(1024)(128)(2,1)S(1)} %reduce.92), channel_id=1, replica_groups=mesh['rep'=4,'seq'=8] {'seq'}, use_global_device_ids=true, to_apply=%region_36.37 | all-reduce | flops 13824 | bytes 55296 | tf_op jit(solution)/shard_map/psum | solution.py:342
  1013.5 85.6 %reduce-scatter.23.cloned.1.call-done = bf16[576,1152]{1,0:T(8,128)(2,1)} async-done(((bf16[4608,1152]{1,0:T(8,128)(2,1)}), bf16[576,1152]{1,0:T(8,128)(2,1)}) %reduce-scatter.23.cloned.1.call-update) | async-done | bytes 1327120 | tf_op jit(solution)/shard_map/reduce_scatter | solution.py:280
  1099.0 85.6 %reduce-scatter.13.cloned.1.call-done = bf16[144,4608]{1,0:T(8,128)(2,1)} async-done(((bf16[1152,4608]{1,0:T(8,128)(2,1)}), bf16[144,4608]{1,0:T(8,128)(2,1)}) %reduce-scatter.13.cloned.1.call-update) | async-done | bytes 1327120 | tf_op jit(solution)/shard_map/reduce_scatter | solution.py:280
  1184.6 85.6 %reduce-scatter.15.cloned.1.call-done = bf16[576,1152]{1,0:T(8,128)(2,1)} async-done(((bf16[4608,1152]{1,0:T(8,128)(2,1)}), bf16[576,1152]{1,0:T(8,128)(2,1)}) %reduce-scatter.15.cloned.1.call-update) | async-done | bytes 1327120 | tf_op jit(solution)/shard_map/reduce_scatter | solution.py:280
  1282.5 9.0 fusion.82
  1293.4 5.7 reshape.1451
  1299.1 5.7 reshape.1450
  1314.0 16.3 fusion.263
  1345.0 22.2 %fusion.113 = bf16[32,16,1152]{2,1,0:T(8,128)(2,1)} fusion(f32[32,16,1152]{2,1,0:T(8,128)} %copy-done.40, bf16[4608,1152]{1,0:T(8,128)(2,1)} %constant_dynamic-update-slice_fusion.15, bf16[1152,4608]{1,0:T(8,128)(2,1)} %all-gather.19.cloned.1.call-done, f32[1152]{0:T(1024)S(1)} %copy-done.115, f32[1152]{0:T(1024)S(1)} %copy-done.71, ...), kind=kOutput, calls=%fused_computation.120 | convolution fusion | flops 10897588224 | bytes 24790528 | tf_op jit(solution)/shard_map/csld,de->csle/dot_general | solution.py:53
  1372.0 19.8 %all_to_all.20 = bf16[8,1,4,1,16,1152]{5,4,2,3,1,0:T(8,128)(2,1)S(1)} all-to-all(bf16[8,1,4,1,16,1152]{5,4,2,3,1,0:T(8,128)(2,1)S(1)} %bitcast.421), channel_id=1, replica_groups=mesh['rep'=4,'seq'=8] {'seq'}, dimensions={0} | all-to-all | bytes 2359296 | tf_op jit(solution)/shard_map/all_to_all | solution.py:130
  1398.3 289.3 %all-reduce.5.cloned.1.call-done = (bf16[144,6912]{1,0:T(8,128)(2,1)}, bf16[144,3456]{1,0:T(8,128)(2,1)}, bf16[144,1152]{1,0:T(8,128)(2,1)}, bf16[144,4608]{1,0:...) async-done(((bf16[144,6912]{1,0:T(8,128)(2,1)}, ...) | async-done | bytes 11943952 | tf_op jit(solution)/shard_map/psum | solution.py:360
  (527 shorter events, 367.6 us)
Async XLA Ops:
  7.2 116.4 %all-gather.9.cloned.1.call-start = ((), (), s32[]{:S(2)}) async-start(), calls=%async_computation.13 | async-start | bytes 8957952 | tf_op jit(solution)/shard_map/all_gather | solution.py:80
  7.9 265.4 %all-gather.11.cloned.1.call-start = ((), (), s32[]{:S(2)}) async-start(), calls=%async_computation.14 | async-start | bytes 2985984 | tf_op jit(solution)/shard_map/all_gather | solution.py:81
  8.7 272.2 %all-gather.13.cloned.1.call-start = ((), (), s32[]{:S(2)}) async-start(), calls=%async_computation.15 | async-start | bytes 11943936 | tf_op jit(solution)/shard_map/all_gather | solution.py:82
  9.4 287.5 %all-gather.23.cloned.1.call-start = ((), (), s32[]{:S(2)}) async-start(), calls=%async_computation.20 | async-start | bytes 11943936 | tf_op jit(solution)/shard_map/all_gather | solution.py:92
  10.0 368.8 %all-gather.15.cloned.1.call-start = ((), (), s32[]{:S(2)}) async-start(), calls=%async_computation.16 | async-start | bytes 8957952 | tf_op jit(solution)/shard_map/all_gather | solution.py:80
  10.6 422.8 %all-gather.17.cloned.1.call-start = ((), (), s32[]{:S(2)}) async-start(), calls=%async_computation.17 | async-start | bytes 2985984 | tf_op jit(solution)/shard_map/all_gather | solution.py:81
  11.2 455.6 %all-gather.19.cloned.1.call-start = ((), (), s32[]{:S(2)}) async-start(), calls=%async_computation.18 | async-start | bytes 11943936 | tf_op jit(solution)/shard_map/all_gather | solution.py:82
  11.9 41.4 %collective-permute-start.1 = (bf16[576,1152]{1,0:T(8,128)(2,1)}, bf16[576,1152]{1,0:T(8,128)(2,1)}, u32[]{:S(2)}, u32[]{:S(2)}) collective-permute-start(bf16[576,1152]{1,0:T(8,128)(2,1)} %param.19), channel_id=1, source_target_pairs={{0,1},{1,2},{2,3},{3,4},{4,5},{5,6},{6,7},{7,0},{8,9},{9,10},{10,1... | collective-permute-start | bytes 3981320 | tf_op jit(solution)/shard_map/ppermute | solution.py:17
  12.4 110.2 %collective-permute-start.2 = (bf16[576,1152]{1,0:T(8,128)(2,1)}, bf16[576,1152]{1,0:T(8,128)(2,1)}, u32[]{:S(2)}, u32[]{:S(2)}) collective-permute-start(bf16[576,1152]{1,0:T(8,128)(2,1)} %param.19), channel_id=1, source_target_pairs={{0,7},{1,0},{2,1},{3,2},{4,3},{5,4},{6,5},{7,6},{8,15},{9,8},{10,9... | collective-permute-start | bytes 3981320 | tf_op jit(solution)/shard_map/ppermute | solution.py:20
  18.3 293.6 %all-to-all-start.2 = ((bf16[1,1,4,8,16,1152]{5,4,2,1,0,3:T(8,128)(2,1)}), bf16[1,1,4,8,16,1152]{5,4,2,1,0,3:T(8,128)(2,1)}, u32[]{:S(2)}, u32[]{:S(2)}) async-start(bf16[1,1,4,8,16,1152]{5,4,2,1,0,3:T(8,128)(2,1)} %copy.326), calls=%async_computation.2 | async-start | bytes 2359296 | tf_op jit(solution)/shard_map/all_to_all | solution.py:108
  22.6 509.9 %all-gather.21.cloned.1.call-start = ((), (), s32[]{:S(2)}) async-start(), calls=%async_computation.19 | async-start | bytes 11943936 | tf_op jit(solution)/shard_map/all_gather | solution.py:92
  53.3 70.3 %collective-permute-start.3 = (bf16[576,1152]{1,0:T(8,128)(2,1)}, bf16[576,1152]{1,0:T(8,128)(2,1)}, u32[]{:S(2)}, u32[]{:S(2)}) collective-permute-start(bf16[576,1152]{1,0:T(8,128)(2,1)} %collective-permute-done.1), channel_id=1, source_target_pairs={{0,1},{1,2},{2,3},{3,4},{4,5},{5,6},{6,7},{7,0},{8,9},{9,10},{10,1... | collective-permute-start | bytes 3981320 | tf_op jit(solution)/shard_map/ppermute | solution.py:17
  121.9 151.4 %copy-start.60 = (f32[1152]{0:T(1024)}, f32[1152]{0:T(1024)S(1)}, u32[]{:S(2)}) copy-start(f32[1152]{0:T(1024)S(1)} %get-tuple-element.36) | copy-start | bytes 13828
  121.9 159.0 %copy-start.76 = (f32[1152]{0:T(1024)}, f32[1152]{0:T(1024)S(1)}, u32[]{:S(2)}) copy-start(f32[1152]{0:T(1024)S(1)} %get-tuple-element.31) | copy-start | bytes 13828
  121.9 159.0 %copy-start.119 = (f32[1152]{0:T(1024)}, f32[1152]{0:T(1024)S(1)}, u32[]{:S(2)}) copy-start(f32[1152]{0:T(1024)S(1)} %get-tuple-element.32) | copy-start | bytes 13828
  121.9 193.5 %copy-start.85 = (f32[1152]{0:T(1024)}, f32[1152]{0:T(1024)S(1)}, u32[]{:S(2)}) copy-start(f32[1152]{0:T(1024)S(1)} %get-tuple-element.33) | copy-start | bytes 13828
  122.7 43.8 %collective-permute-start.4 = (bf16[576,1152]{1,0:T(8,128)(2,1)}, bf16[576,1152]{1,0:T(8,128)(2,1)}, u32[]{:S(2)}, u32[]{:S(2)}) collective-permute-start(bf16[576,1152]{1,0:T(8,128)(2,1)} %collective-permute-done.2), channel_id=1, source_target_pairs={{0,7},{1,0},{2,1},{3,2},{4,3},{5,4},{6,5},{7,6},{8,15},{9,8},{10,9... | collective-permute-start | bytes 3981320 | tf_op jit(solution)/shard_map/ppermute | solution.py:20
  123.6 48.2 %collective-permute-start.5 = (bf16[576,1152]{1,0:T(8,128)(2,1)}, bf16[576,1152]{1,0:T(8,128)(2,1)}, u32[]{:S(2)}, u32[]{:S(2)}) collective-permute-start(bf16[576,1152]{1,0:T(8,128)(2,1)} %collective-permute-done.3), channel_id=1, source_target_pairs={{0,1},{1,2},{2,3},{3,4},{4,5},{5,6},{6,7},{7,0},{8,9},{9,10},{10,1... | collective-permute-start | bytes 3981320 | tf_op jit(solution)/shard_map/ppermute | solution.py:17
  136.2 97.8 %collective-permute-start = (bf16[2,1,4,128,1152]{4,3,2,1,0:T(8,128)(2,1)}, bf16[2,1,4,128,1152]{4,3,2,1,0:T(8,128)(2,1)}, u32[]{:S(2)}, u32[]{:S(2)}) collective-permute-start(bf16[2,1,4,128,1152]{4,3,2,1,0:T(8,128)(2,1)} %pad_maximum_fusion.1), channel_id=1, source_target_pairs={{0,1},{1,0},{2,3},{3,2},{4,5},{5,4},{6,7},{7,6},{8,9},{9,8},{10,11... | collective-permute-start | bytes 7077896 | tf_op jit(solution)/shard_map/ppermute | solution.py:34
  136.3 242.5 %copy-start.116 = (f32[1152]{0:T(1024)}, f32[1152]{0:T(1024)S(1)}, u32[]{:S(2)}) copy-start(f32[1152]{0:T(1024)S(1)} %get-tuple-element.28) | copy-start | bytes 13828
  136.3 330.5 %copy-start.113 = (f32[1152]{0:T(1024)}, f32[1152]{0:T(1024)S(1)}, u32[]{:S(2)}) copy-start(f32[1152]{0:T(1024)S(1)} %get-tuple-element.26) | copy-start | bytes 13828
  136.3 396.2 %copy-start.82 = (f32[1152]{0:T(1024)}, f32[1152]{0:T(1024)S(1)}, u32[]{:S(2)}) copy-start(f32[1152]{0:T(1024)S(1)} %get-tuple-element.25) | copy-start | bytes 13828
  136.3 426.0 %copy-start.69 = (f32[1152]{0:T(1024)}, f32[1152]{0:T(1024)S(1)}, u32[]{:S(2)}) copy-start(f32[1152]{0:T(1024)S(1)} %get-tuple-element.27) | copy-start | bytes 13828
  136.3 428.3 %copy-start.72 = (f32[1152]{0:T(1024)}, f32[1152]{0:T(1024)S(1)}, u32[]{:S(2)}) copy-start(f32[1152]{0:T(1024)S(1)} %get-tuple-element.30) | copy-start | bytes 13828
  136.3 551.0 %copy-start.74 = (f32[1152]{0:T(1024)}, f32[1152]{0:T(1024)S(1)}, u32[]{:S(2)}) copy-start(f32[1152]{0:T(1024)S(1)} %get-tuple-element.29) | copy-start | bytes 13828
  166.5 53.4 %collective-permute-start.6 = (bf16[576,1152]{1,0:T(8,128)(2,1)}, bf16[576,1152]{1,0:T(8,128)(2,1)S(1)}, u32[]{:S(2)}, u32[]{:S(2)}) collective-permute-start(bf16[576,1152]{1,0:T(8,128)(2,1)} %collective-permute-done.4), channel_id=1, source_target_pairs={{0,7},{1,0},{2,1},{3,2},{4,3},{5,4},{6,5},{7,6},{8,15},{9,8},{10,9... | collective-permute-start | bytes 3981320 | tf_op jit(solution)/shard_map/ppermute | solution.py:20
  171.8 53.9 %collective-permute-start.7 = (bf16[576,1152]{1,0:T(8,128)(2,1)}, bf16[576,1152]{1,0:T(8,128)(2,1)S(1)}, u32[]{:S(2)}, u32[]{:S(2)}) collective-permute-start(bf16[576,1152]{1,0:T(8,128)(2,1)} %collective-permute-done.5), channel_id=1, source_target_pairs={{0,1},{1,2},{2,3},{3,4},{4,5},{5,6},{6,7},{7,0},{8,9},{9,10},{10,1... | collective-permute-start | bytes 3981320 | tf_op jit(solution)/shard_map/ppermute | solution.py:17
  311.8 21.5 %all-to-all-start.3 = ((bf16[1,1,4,8,16,1152]{5,4,2,1,0,3:T(8,128)(2,1)}), bf16[1,1,4,8,16,1152]{5,4,2,1,0,3:T(8,128)(2,1)S(1)}, u32[]{:S(2)}, u32[]{:S(2)}) async-start(bf16[1,1,4,8,16,1152]{5,4,2,1,0,3:T(8,128)(2,1)} %copy.329), calls=%async_computation.3 | async-start | bytes 2359296 | tf_op jit(solution)/shard_map/all_to_all | solution.py:108
  333.3 34.2 %all-to-all-start = ((bf16[1,1,4,8,16,1152]{5,4,2,1,0,3:T(8,128)(2,1)}), bf16[1,1,4,8,16,1152]{5,4,2,1,0,3:T(8,128)(2,1)}, u32[]{:S(2)}, u32[]{:S(2)}) async-start(bf16[1,1,4,8,16,1152]{5,4,2,1,0,3:T(8,128)(2,1)} %copy.309), calls=%async_computation | async-start | bytes 2359296 | tf_op jit(solution)/shard_map/all_to_all | solution.py:108
  440.6 121.7 %copy-start.62 = (f32[32,16]{1,0:T(8,128)}, f32[32,16]{1,0:T(8,128)S(1)}, u32[]{:S(2)}) copy-start(f32[32,16]{1,0:T(8,128)S(1)} %broadcast_multiply_fusion) | copy-start | bytes 6148
  627.6 20.3 %all-to-all-start.4 = ((bf16[8,1,4,1,16,1152]{5,4,2,3,1,0:T(8,128)(2,1)}), bf16[8,1,4,1,16,1152]{5,4,2,3,1,0:T(8,128)(2,1)S(1)}, u32[]{:S(2)}, u32[]{:S(2)}) async-start(bf16[8,1,4,1,16,1152]{5,4,2,3,1,0:T(8,128)(2,1)} %bitcast.419), calls=%async_computation.4 | async-start | bytes 2359296 | tf_op jit(solution)/shard_map/all_to_all | solution.py:130
  631.2 381.0 %reduce-scatter.19.cloned.1.call-start = ((), (), s32[]{:S(2)}) async-start(), calls=%async_computation.26 | async-start | bytes 2985984 | tf_op jit(solution)/shard_map/reduce_scatter | solution.py:280
  643.9 368.3 %reduce-scatter.11.cloned.1.call-start = ((), (), s32[]{:S(2)}) async-start(), calls=%async_computation.22 | async-start | bytes 2985984 | tf_op jit(solution)/shard_map/reduce_scatter | solution.py:280
  687.2 325.0 %reduce-scatter.17.cloned.1.call-start = ((), (), s32[]{:S(2)}) async-start(), calls=%async_computation.25 | async-start | bytes 8957952 | tf_op jit(solution)/shard_map/reduce_scatter | solution.py:280
  698.5 313.7 %reduce-scatter.9.cloned.1.call-start = ((), (), s32[]{:S(2)}) async-start(), calls=%async_computation.21 | async-start | bytes 8957952 | tf_op jit(solution)/shard_map/reduce_scatter | solution.py:280
  743.7 4.9 collective-permute-start.15
  771.1 242.4 %reduce-scatter.21.cloned.1.call-start = ((), (), s32[]{:S(2)}) async-start(), calls=%async_computation.27 | async-start | bytes 11943936 | tf_op jit(solution)/shard_map/reduce_scatter | solution.py:280
  783.2 315.8 %reduce-scatter.23.cloned.1.call-start = ((), (), s32[]{:S(2)}) async-start(), calls=%async_computation.28 | async-start | bytes 11943936 | tf_op jit(solution)/shard_map/reduce_scatter | solution.py:280
  799.2 385.4 %reduce-scatter.13.cloned.1.call-start = ((), (), s32[]{:S(2)}) async-start(), calls=%async_computation.23 | async-start | bytes 11943936 | tf_op jit(solution)/shard_map/reduce_scatter | solution.py:280
  810.9 459.3 %reduce-scatter.15.cloned.1.call-start = ((), (), s32[]{:S(2)}) async-start(), calls=%async_computation.24 | async-start | bytes 11943936 | tf_op jit(solution)/shard_map/reduce_scatter | solution.py:280
  825.0 862.6 %all-reduce.5.cloned.1.call-start = ((), (), s32[]{:S(2)}) async-start(), calls=%async_computation.29 | async-start | bytes 23887872 | tf_op jit(solution)/shard_map/psum | solution.py:360
  826.6 46.2 %collective-permute-start.8 = (bf16[576,1152]{1,0:T(8,128)(2,1)S(1)}, bf16[576,1152]{1,0:T(8,128)(2,1)S(1)}, u32[]{:S(2)}, u32[]{:S(2)}) collective-permute-start(bf16[576,1152]{1,0:T(8,128)(2,1)S(1)} %copy-done.36), channel_id=1, source_target_pairs={{0,1},{1,2},{2,3},{3,4},{4,5},{5,6},{6,7},{7,0},{8,9},{9,10},{10,1... | collective-permute-start | bytes 3981320 | tf_op jit(solution)/shard_map/ppermute | solution.py:17
  826.6 49.3 %collective-permute-start.9 = (bf16[576,1152]{1,0:T(8,128)(2,1)S(1)}, bf16[576,1152]{1,0:T(8,128)(2,1)}, u32[]{:S(2)}, u32[]{:S(2)}) collective-permute-start(bf16[576,1152]{1,0:T(8,128)(2,1)S(1)} %copy-done.36), channel_id=1, source_target_pairs={{0,7},{1,0},{2,1},{3,2},{4,3},{5,4},{6,5},{7,6},{8,15},{9,8},{10,9... | collective-permute-start | bytes 3981320 | tf_op jit(solution)/shard_map/ppermute | solution.py:20
  872.8 45.5 %collective-permute-start.10 = (bf16[576,1152]{1,0:T(8,128)(2,1)S(1)}, bf16[576,1152]{1,0:T(8,128)(2,1)}, u32[]{:S(2)}, u32[]{:S(2)}) collective-permute-start(bf16[576,1152]{1,0:T(8,128)(2,1)S(1)} %collective-permute-done.8), channel_id=1, source_target_pairs={{0,1},{1,2},{2,3},{3,4},{4,5},{5,6},{6,7},{7,0},{8,9},{9,10},{10,1... | collective-permute-start | bytes 3981320 | tf_op jit(solution)/shard_map/ppermute | solution.py:17
  875.9 43.5 %collective-permute-start.11 = (bf16[576,1152]{1,0:T(8,128)(2,1)}, bf16[576,1152]{1,0:T(8,128)(2,1)}, u32[]{:S(2)}, u32[]{:S(2)}) collective-permute-start(bf16[576,1152]{1,0:T(8,128)(2,1)} %collective-permute-done.9), channel_id=1, source_target_pairs={{0,7},{1,0},{2,1},{3,2},{4,3},{5,4},{6,5},{7,6},{8,15},{9,8},{10,9... | collective-permute-start | bytes 3981320 | tf_op jit(solution)/shard_map/ppermute | solution.py:20
  918.2 32.8 %collective-permute-start.12 = (bf16[576,1152]{1,0:T(8,128)(2,1)}, bf16[576,1152]{1,0:T(8,128)(2,1)}, u32[]{:S(2)}, u32[]{:S(2)}) collective-permute-start(bf16[576,1152]{1,0:T(8,128)(2,1)} %collective-permute-done.10), channel_id=1, source_target_pairs={{0,1},{1,2},{2,3},{3,4},{4,5},{5,6},{6,7},{7,0},{8,9},{9,10},{10,1... | collective-permute-start | bytes 3981320 | tf_op jit(solution)/shard_map/ppermute | solution.py:17
  919.4 33.1 %collective-permute-start.13 = (bf16[576,1152]{1,0:T(8,128)(2,1)}, bf16[576,1152]{1,0:T(8,128)(2,1)S(1)}, u32[]{:S(2)}, u32[]{:S(2)}) collective-permute-start(bf16[576,1152]{1,0:T(8,128)(2,1)} %collective-permute-done.11), channel_id=1, source_target_pairs={{0,7},{1,0},{2,1},{3,2},{4,3},{5,4},{6,5},{7,6},{8,15},{9,8},{10,9... | collective-permute-start | bytes 3981320 | tf_op jit(solution)/shard_map/ppermute | solution.py:20
  951.0 319.3 %collective-permute-start.14 = (bf16[576,1152]{1,0:T(8,128)(2,1)}, bf16[576,1152]{1,0:T(8,128)(2,1)}, u32[]{:S(2)}, u32[]{:S(2)}) collective-permute-start(bf16[576,1152]{1,0:T(8,128)(2,1)} %collective-permute-done.12), channel_id=1, source_target_pairs={{0,1},{1,2},{2,3},{3,4},{4,5},{5,6},{6,7},{7,0},{8,9},{9,10},{10,1... | collective-permute-start | bytes 3981320 | tf_op jit(solution)/shard_map/ppermute | solution.py:17
  (117 other events, 1072.1 us)
Sparse Core Ops, SparseCore 0:
  9.9 86.2 all-gather.8
  98.1 32.8 all-gather.10
  132.9 95.9 all-gather.12
  230.6 66.2 all-gather.22
  298.6 70.5 all-gather.14
  371.0 30.0 all-gather.16
  402.9 63.8 all-gather.18
  468.6 63.8 all-gather.20
  644.0 45.1 reduce-scatter.18
  693.5 43.7 reduce-scatter.10
  740.8 70.0 reduce-scatter.16
  814.7 100.5 reduce-scatter.8
  918.8 94.6 reduce-scatter.20
  1016.8 82.1 reduce-scatter.22
  1102.4 82.1 reduce-scatter.12
  1188.0 82.2 reduce-scatter.14
  1275.1 412.4 all-reduce.4
